TPU v7x, 32 devices: a whole 2x2x4 slice. The times are simulated.
32 devices in a mesh: section: 2 (over x), expert: 16 (over z, y, core).
Axes of the slice: x: 2, y: 2, z: 4, core: 2. Of those that a mesh axis runs over, the one named last changes fastest.
Arguments:
- hidden_in: bfloat16 [2, 128, 3584], P(None, 'expert'), may hold values from -6 to 6
- layer_gain: float32 [2, 3584], P('section'), may hold values from 0.25 to 1.75
- router: bfloat16 [2, 3584, 4], P('section'), may hold values from -0.09375 to 0.09375
- w_gate: bfloat16 [2, 3584, 8192], P('section', None, 'expert'), may hold values from -0.09375 to 0.09375
- w_up: bfloat16 [2, 3584, 8192], P('section', None, 'expert'), may hold values from -0.09375 to 0.09375
- w_down: bfloat16 [2, 8192, 3584], P('section', 'expert'), may hold values from -0.125 to 0.125
- final_gain: float32 [3584], replicated, may hold values from 0.25 to 1.75
- head: bfloat16 [8192, 3584], P(('section', 'expert')), may hold values from -18.775102 to 18.775102
- routing: int32 [2, 2, 128, 2], P('section', None, 'expert'), may hold values from 0 to 3, all different within a row; in each aligned block of 8 rows (0 to 7, 8 to 15, ..., all dimensions but the last counted through in order) at most 4 rows name the same one
- targets: int32 [2, 128], replicated, may hold values from 0 to 8191
- seq_ids: int32 [2, 128], replicated, may hold values from 0 to 3, never falling along the last dimension, each value on 1 to 64 neighbouring positions
Outputs:
- token_logprob: float32 [2, 128], P(None, 'expert')
- seq_mean: float32 [2, 4], replicated
Inputs may be any that keep to these rules, and one draw needn't show every extreme that they name: `routing`: in each aligned block of 8 tokens (the tokens of one device) a token's 2 experts differ and no expert is named by more than 4 tokens; some expert is named by exactly 4. `seq_ids`: ids never fall along a micro-batch's tokens; each of the 4 ids occurs on 1 to 64 tokens, one on exactly 64.
All inputs are finite; a program needn't handle non-finite values.
Results may differ from a plain program's by a relative error of at most 0.014.
Values may be sent and summed in bfloat16 or wider, within the bound.
A program may use at most 64 MiB of HBM per device.

v0:
```python
import jax
import jax.numpy as jnp
from jax import lax
from jax.sharding import PartitionSpec as P

SEQS = 4


def shifted(shard, axis, by):
    size = lax.axis_size(axis)
    pairs = [(i, i + by) for i in range(size) if 0 <= i + by < size]
    return lax.ppermute(shard, axis, pairs)


def broadcast(block, axis, holder):
    block = jnp.where(lax.axis_index(axis) == holder, block, jnp.zeros_like(block))
    return lax.psum(block, axis)


def rms_scale(states, gain):
    values = states.astype(jnp.float32)
    factor = lax.rsqrt(jnp.mean(values * values, -1, keepdims=True) + 1e-06)
    return values * factor * gain


def body(
    hidden_in, layer_gain, router, w_gate, w_up, w_down, final_gain, head, routing, targets, seq_ids
):
    micro_count, tok_count, model_width = hidden_in.shape
    expert_count = router.shape[2]
    top_count = routing.shape[3]
    sections = lax.axis_size("section")
    members = lax.axis_size("expert")
    section_pos = lax.axis_index("section")
    member_pos = lax.axis_index("expert")
    split_count = members // expert_count
    capacity = min(tok_count, 9 * tok_count * top_count // (8 * expert_count))
    tick_count = micro_count + sections - 1

    def expert_rows(incoming):
        sources, slot_count, width_in = incoming.shape
        flat_rows = incoming.reshape(sources * slot_count, width_in)
        gate_val = jnp.dot(flat_rows, w_gate[0], preferred_element_type=jnp.float32)
        up_val = jnp.dot(flat_rows, w_up[0], preferred_element_type=jnp.float32)
        inner = (jax.nn.silu(gate_val) * up_val).astype(jnp.bfloat16)
        partial_value = jnp.dot(inner, w_down[0], preferred_element_type=jnp.float32).astype(
            jnp.bfloat16
        )
        return lax.all_to_all(
            partial_value.reshape(sources, slot_count, width_in),
            "expert",
            split_axis=0,
            concat_axis=0,
            tiled=True,
        )

    def expert_layer(states, micro_pos):
        route_ids = lax.dynamic_index_in_dim(routing[0], micro_pos, 0, keepdims=False)
        normed = rms_scale(states, layer_gain[0]).astype(jnp.bfloat16)
        logits = jnp.dot(normed, router[0], preferred_element_type=jnp.float32)
        chosen = route_ids[:, :, None] == jnp.arange(expert_count, dtype=jnp.int32)[None, None, :]
        affinity = jax.nn.sigmoid(jnp.sum(jnp.where(chosen, logits[:, None, :], 0.0), -1))
        weight = affinity / jnp.sum(affinity, -1, keepdims=True)
        flags = chosen.reshape(tok_count * top_count, expert_count).astype(jnp.int32)
        ranks = jnp.cumsum(flags, 0) - flags
        slot_ids = jnp.sum(ranks * flags, -1).reshape(tok_count, top_count)
        destination = route_ids * capacity + slot_ids
        places = jnp.arange(expert_count * capacity, dtype=jnp.int32)
        table = jnp.any(places[:, None, None] == destination[None], -1).astype(jnp.bfloat16)
        packed = jnp.dot(table, normed, preferred_element_type=jnp.float32).astype(jnp.bfloat16)
        outgoing = jnp.broadcast_to(
            packed.reshape(expert_count, 1, capacity, model_width),
            (expert_count, split_count, capacity, model_width),
        )
        outgoing = outgoing.reshape(members, capacity, model_width)
        returned = expert_rows(
            lax.all_to_all(outgoing, "expert", split_axis=0, concat_axis=0, tiled=True)
        )
        summed = jnp.sum(
            returned.reshape(expert_count, split_count, capacity, model_width).astype(jnp.float32),
            1,
        )
        summed = summed.reshape(expert_count * capacity, model_width)
        picked = summed[destination]
        mixed = jnp.sum(weight[:, :, None] * picked, 1)
        return (states.astype(jnp.float32) + 2.5 * mixed).astype(jnp.bfloat16)

    def advance(step, carry):
        arrived, record = carry
        entering = lax.dynamic_index_in_dim(
            hidden_in, jnp.minimum(step, micro_count - 1), 0, keepdims=False
        )
        states = jnp.where(section_pos == 0, entering, arrived)
        micro_pos = jnp.clip(step - section_pos, 0, micro_count - 1)
        result = expert_layer(states, micro_pos)
        finished = step - (sections - 1)
        record_pos = jnp.clip(finished, 0, micro_count - 1)
        keeping = (finished >= 0) & (section_pos == sections - 1)
        previous = lax.dynamic_index_in_dim(record, record_pos, 0, keepdims=False)
        record = lax.dynamic_update_index_in_dim(
            record, jnp.where(keeping, result, previous), record_pos, 0
        )
        arrived = shifted(result, "section", 1)
        return (arrived, record)

    start_rows = jnp.zeros((tok_count, model_width), jnp.bfloat16)
    start_record = jnp.zeros((micro_count, tok_count, model_width), jnp.bfloat16)
    arrived, record = lax.fori_loop(0, tick_count, advance, (start_rows, start_record))
    shared = broadcast(record, "section", sections - 1)
    normed = rms_scale(lax.all_gather(shared, "expert", axis=1, tiled=True), final_gain).astype(
        jnp.bfloat16
    )
    logits = jnp.einsum("mrd,vd->mrv", normed, head, preferred_element_type=jnp.float32)
    voc_count = head.shape[0]
    vocab_start = (section_pos * members + member_pos) * voc_count
    vocab_ids = vocab_start + jnp.arange(voc_count, dtype=jnp.int32)
    target_hit = targets[:, :, None] == vocab_ids[None, None, :]
    target_part = jnp.sum(jnp.where(target_hit, logits, 0.0), -1)
    local_max = jnp.max(logits, -1)
    peak = lax.pmax(local_max, ("section", "expert"))
    local_sum = jnp.sum(jnp.exp(logits - peak[..., None]), -1)
    total, target_logit = lax.psum((local_sum, target_part), ("section", "expert"))
    logprob = target_logit - (peak + jnp.log(total))
    token_part = lax.dynamic_slice_in_dim(logprob, member_pos * tok_count, tok_count, 1)
    member = seq_ids[:, :, None] == jnp.arange(SEQS, dtype=jnp.int32)[None, None, :]
    sums = jnp.sum(jnp.where(member, logprob[..., None], 0.0), 1)
    counts = jnp.sum(member.astype(jnp.float32), 1)
    return (token_part, sums / counts)


def solution(mesh):
    return jax.shard_map(
        body,
        mesh=mesh,
        in_specs=(
            P(None, "expert", None),
            P("section", None),
            P("section", None, None),
            P("section", None, "expert"),
            P("section", None, "expert"),
            P("section", "expert", None),
            P(),
            P(("section", "expert"), None),
            P("section", None, "expert", None),
            P(),
            P(),
        ),
        out_specs=(P(None, "expert"), P()),
        check_vma=False,
    )
```

profile of v0, /device:TPU:0, one launch (start us, length us, event | category | flops | bytes accessed | tf_op | source)
XLA Modules:
  0.0 332.3 jit_solution(14966221587501759313)
XLA Ops:
  7.3 167.9 %while.17 = (s32[]{:T(128)}, bf16[8,3584]{1,0:T(8,128)(2,1)S(1)}, bf16[2,8,3584]{2,1,0:T(8,128)(2,1)S(1)}, pred[]{:T(512)}, bf16[2,8,3584]{2,1,0:T(8,128)(2,1)},...) while((s32[]{:T(128)}, bf16[8,3584]{1,0:T(8,128)(2,1)S(1)}, ...), condition=%wide.region_9.10_spmd, body=%wide.region_0.9_spmd.sunk | while | flops 707251328 | bytes 21631636 | solution.py:108
  7.3 0.8 constant_dynamic-slice_fusion.6
  8.7 0.7 multiply_add_fusion.2
  9.5 1.0 fusion.70
  10.5 0.8 reduce.2
  11.5 0.9 broadcast_in_dim.134
  12.4 7.4 %all-to-all-start = ((bf16[16,4,3584]{2,1,0:T(4,128)(2,1)}), bf16[16,4,3584]{2,1,0:T(4,128)(2,1)S(1)}, u32[]{:S(2)}, u32[]{:S(2)}) async-start(bf16[16,4,3584]{2,1,0:T(4,128)(2,1)} %bitcast.77), calls=%async_computation | async-start | bytes 917504 | tf_op jit(solution)/shard_map/while/body/eval_jaxpr/all_to_all | solution.py:77
  20.0 0.7 compare_select_fusion.2
  20.8 0.7 fusion.73
  21.5 0.9 fusion.72
  22.5 10.5 %all-to-all-done = bf16[16,4,3584]{2,1,0:T(4,128)(2,1)S(1)} async-done(((bf16[16,4,3584]{2,1,0:T(4,128)(2,1)}), bf16[16,4,3584]{2,1,0:T(4,128)(2,1)S(1)}, u32[]{:S(2)}, u32[]{:S(2)}) %all-to-all-start) | async-done | bytes 458784 | tf_op jit(solution)/shard_map/while/body/eval_jaxpr/all_to_all | solution.py:77
  33.2 2.8 fusion.71
  35.9 4.6 %convolution_convert_fusion.5 = bf16[64,3584]{1,0:T(8,128)(2,1)S(1)} fusion(bf16[1,512,3584]{2,1,0:T(8,128)(2,1)} %get-tuple-element.450, bf16[64,3584]{1,0:T(8,128)(2,1)S(1)} %reshape.218, bf16[1,3584,512]{2,1,0:T(8,128)(2,1)} %get-tuple-element.449, f32[64,512]{1,0:T(8,128)S(1)} %fusion.71), kind=kOutput, calls=%fused_computation.1.clone.1 | convolution fusion | flops 470188032 | bytes 8388608 | tf_op jit(solution)/shard_map/while/body/eval_jaxpr/dot_general | solution.py:46
  40.6 0.9 reshape.219
  41.4 3.8 %all-to-all-start.1 = ((bf16[16,4,3584]{2,1,0:T(4,128)(2,1)}), bf16[16,4,3584]{2,1,0:T(4,128)(2,1)S(1)}, u32[]{:S(2)}, u32[]{:S(2)}) async-start(bf16[16,4,3584]{2,1,0:T(4,128)(2,1)} %reshape.219), calls=%async_computation.1 | async-start | bytes 917504 | tf_op jit(solution)/shard_map/while/body/eval_jaxpr/all_to_all | solution.py:49
  45.4 13.1 %all-to-all-done.1 = bf16[16,4,3584]{2,1,0:T(4,128)(2,1)S(1)} async-done(((bf16[16,4,3584]{2,1,0:T(4,128)(2,1)}), bf16[16,4,3584]{2,1,0:T(4,128)(2,1)S(1)}, u32[]{:S(2)}, u32[]{:S(2)}) %all-to-all-start.1) | async-done | bytes 458784 | tf_op jit(solution)/shard_map/while/body/eval_jaxpr/all_to_all | solution.py:49
  58.8 0.6 gather_fusion
  59.9 3.4 %collective-permute-start = (bf16[8,3584]{1,0:T(8,128)(2,1)S(1)}, bf16[8,3584]{1,0:T(8,128)(2,1)S(1)}, u32[]{:S(2)}, u32[]{:S(2)}) collective-permute-start(bf16[8,3584]{1,0:T(8,128)(2,1)S(1)} %get-tuple-element.401), channel_id=1, source_target_pairs={{0,16},{1,17},{2,18},{3,19},{4,20},{5,21},{6,22},{7,23},{8,24},{9,... | collective-permute-start | bytes 172040 | tf_op jit(solution)/shard_map/while/body/eval_jaxpr/ppermute | solution.py:12
  63.4 1.8 collective-permute-done
  65.2 0.7 constant_dynamic-slice_fusion.6
  66.5 0.7 multiply_add_fusion.2
  67.2 1.0 fusion.70
  68.2 0.8 reduce.2
  69.3 0.9 broadcast_in_dim.134
  70.1 3.8 %all-to-all-start = ((bf16[16,4,3584]{2,1,0:T(4,128)(2,1)}), bf16[16,4,3584]{2,1,0:T(4,128)(2,1)S(1)}, u32[]{:S(2)}, u32[]{:S(2)}) async-start(bf16[16,4,3584]{2,1,0:T(4,128)(2,1)} %bitcast.77), calls=%async_computation | async-start | bytes 917504 | tf_op jit(solution)/shard_map/while/body/eval_jaxpr/all_to_all | solution.py:77
  74.1 0.7 compare_select_fusion.2
  75.0 0.7 fusion.73
  75.6 0.9 fusion.72
  76.6 10.5 %all-to-all-done = bf16[16,4,3584]{2,1,0:T(4,128)(2,1)S(1)} async-done(((bf16[16,4,3584]{2,1,0:T(4,128)(2,1)}), bf16[16,4,3584]{2,1,0:T(4,128)(2,1)S(1)}, u32[]{:S(2)}, u32[]{:S(2)}) %all-to-all-start) | async-done | bytes 458784 | tf_op jit(solution)/shard_map/while/body/eval_jaxpr/all_to_all | solution.py:77
  87.3 2.8 fusion.71
  90.1 4.6 %convolution_convert_fusion.5 = bf16[64,3584]{1,0:T(8,128)(2,1)S(1)} fusion(bf16[1,512,3584]{2,1,0:T(8,128)(2,1)} %get-tuple-element.450, bf16[64,3584]{1,0:T(8,128)(2,1)S(1)} %reshape.218, bf16[1,3584,512]{2,1,0:T(8,128)(2,1)} %get-tuple-element.449, f32[64,512]{1,0:T(8,128)S(1)} %fusion.71), kind=kOutput, calls=%fused_computation.1.clone.1 | convolution fusion | flops 470188032 | bytes 8388608 | tf_op jit(solution)/shard_map/while/body/eval_jaxpr/dot_general | solution.py:46
  94.7 0.9 reshape.219
  95.6 3.8 %all-to-all-start.1 = ((bf16[16,4,3584]{2,1,0:T(4,128)(2,1)}), bf16[16,4,3584]{2,1,0:T(4,128)(2,1)S(1)}, u32[]{:S(2)}, u32[]{:S(2)}) async-start(bf16[16,4,3584]{2,1,0:T(4,128)(2,1)} %reshape.219), calls=%async_computation.1 | async-start | bytes 917504 | tf_op jit(solution)/shard_map/while/body/eval_jaxpr/all_to_all | solution.py:49
  99.5 13.1 %all-to-all-done.1 = bf16[16,4,3584]{2,1,0:T(4,128)(2,1)S(1)} async-done(((bf16[16,4,3584]{2,1,0:T(4,128)(2,1)}), bf16[16,4,3584]{2,1,0:T(4,128)(2,1)S(1)}, u32[]{:S(2)}, u32[]{:S(2)}) %all-to-all-start.1) | async-done | bytes 458784 | tf_op jit(solution)/shard_map/while/body/eval_jaxpr/all_to_all | solution.py:49
  112.9 0.6 gather_fusion
  114.1 4.3 %collective-permute-start = (bf16[8,3584]{1,0:T(8,128)(2,1)S(1)}, bf16[8,3584]{1,0:T(8,128)(2,1)S(1)}, u32[]{:S(2)}, u32[]{:S(2)}) collective-permute-start(bf16[8,3584]{1,0:T(8,128)(2,1)S(1)} %get-tuple-element.401), channel_id=1, source_target_pairs={{0,16},{1,17},{2,18},{3,19},{4,20},{5,21},{6,22},{7,23},{8,24},{9,... | collective-permute-start | bytes 172040 | tf_op jit(solution)/shard_map/while/body/eval_jaxpr/ppermute | solution.py:12
  118.4 1.8 collective-permute-done
  120.2 0.7 constant_dynamic-slice_fusion.6
  121.5 0.7 multiply_add_fusion.2
  122.3 1.0 fusion.70
  123.2 0.8 reduce.2
  124.3 0.9 broadcast_in_dim.134
  125.2 3.8 %all-to-all-start = ((bf16[16,4,3584]{2,1,0:T(4,128)(2,1)}), bf16[16,4,3584]{2,1,0:T(4,128)(2,1)S(1)}, u32[]{:S(2)}, u32[]{:S(2)}) async-start(bf16[16,4,3584]{2,1,0:T(4,128)(2,1)} %bitcast.77), calls=%async_computation | async-start | bytes 917504 | tf_op jit(solution)/shard_map/while/body/eval_jaxpr/all_to_all | solution.py:77
  129.1 0.7 compare_select_fusion.2
  130.0 0.7 fusion.73
  130.7 0.9 fusion.72
  131.7 10.5 %all-to-all-done = bf16[16,4,3584]{2,1,0:T(4,128)(2,1)S(1)} async-done(((bf16[16,4,3584]{2,1,0:T(4,128)(2,1)}), bf16[16,4,3584]{2,1,0:T(4,128)(2,1)S(1)}, u32[]{:S(2)}, u32[]{:S(2)}) %all-to-all-start) | async-done | bytes 458784 | tf_op jit(solution)/shard_map/while/body/eval_jaxpr/all_to_all | solution.py:77
  142.3 2.8 fusion.71
  145.1 4.6 %convolution_convert_fusion.5 = bf16[64,3584]{1,0:T(8,128)(2,1)S(1)} fusion(bf16[1,512,3584]{2,1,0:T(8,128)(2,1)} %get-tuple-element.450, bf16[64,3584]{1,0:T(8,128)(2,1)S(1)} %reshape.218, bf16[1,3584,512]{2,1,0:T(8,128)(2,1)} %get-tuple-element.449, f32[64,512]{1,0:T(8,128)S(1)} %fusion.71), kind=kOutput, calls=%fused_computation.1.clone.1 | convolution fusion | flops 470188032 | bytes 8388608 | tf_op jit(solution)/shard_map/while/body/eval_jaxpr/dot_general | solution.py:46
  149.7 0.9 reshape.219
  150.6 3.8 %all-to-all-start.1 = ((bf16[16,4,3584]{2,1,0:T(4,128)(2,1)}), bf16[16,4,3584]{2,1,0:T(4,128)(2,1)S(1)}, u32[]{:S(2)}, u32[]{:S(2)}) async-start(bf16[16,4,3584]{2,1,0:T(4,128)(2,1)} %reshape.219), calls=%async_computation.1 | async-start | bytes 917504 | tf_op jit(solution)/shard_map/while/body/eval_jaxpr/all_to_all | solution.py:49
  154.5 13.1 %all-to-all-done.1 = bf16[16,4,3584]{2,1,0:T(4,128)(2,1)S(1)} async-done(((bf16[16,4,3584]{2,1,0:T(4,128)(2,1)}), bf16[16,4,3584]{2,1,0:T(4,128)(2,1)S(1)}, u32[]{:S(2)}, u32[]{:S(2)}) %all-to-all-start.1) | async-done | bytes 458784 | tf_op jit(solution)/shard_map/while/body/eval_jaxpr/all_to_all | solution.py:49
  167.9 0.6 gather_fusion
  169.1 4.3 %collective-permute-start = (bf16[8,3584]{1,0:T(8,128)(2,1)S(1)}, bf16[8,3584]{1,0:T(8,128)(2,1)S(1)}, u32[]{:S(2)}, u32[]{:S(2)}) collective-permute-start(bf16[8,3584]{1,0:T(8,128)(2,1)S(1)} %get-tuple-element.401), channel_id=1, source_target_pairs={{0,16},{1,17},{2,18},{3,19},{4,20},{5,21},{6,22},{7,23},{8,24},{9,... | collective-permute-start | bytes 172040 | tf_op jit(solution)/shard_map/while/body/eval_jaxpr/ppermute | solution.py:12
  173.4 1.8 collective-permute-done
  175.2 0.6 broadcast_select_fusion
  175.9 21.4 %all-reduce.3.cloned.1.call-done = bf16[2,8,3584]{2,1,0:T(8,128)(2,1)} async-done(((bf16[2,8,3584]{2,1,0:T(8,128)(2,1)}), bf16[2,8,3584]{2,1,0:T(8,128)(2,1)}) %all-reduce.3.cloned.1.call-update) | async-done | bytes 114704 | tf_op jit(solution)/shard_map/psum | solution.py:17
  197.5 42.9 %all-gather.2.cloned.1.call-done = bf16[2,128,3584]{2,1,0:T(8,128)(2,1)} async-done(((bf16[2,8,3584]{2,1,0:T(8,128)(2,1)}), bf16[2,128,3584]{2,1,0:T(8,128)(2,1)}) %all-gather.2.cloned.1.call-update) | async-done | bytes 1835024 | tf_op jit(solution)/shard_map/all_gather | solution.py:110
  240.4 1.9 fusion.30
  242.4 2.3 fusion.39
  244.6 38.4 %pmax.7 = f32[2,128]{1,0:T(2,128)S(1)} all-reduce(f32[2,128]{1,0:T(2,128)S(1)} %get-tuple-element.314), channel_id=1, replica_groups=mesh['section'=2,'expert'=16] {'section','expert'}, use_global_device_ids=true, to_apply=%region_15.16 | all-reduce | flops 256 | bytes 2048 | tf_op jit(solution)/shard_map/pmax | solution.py:120
  283.3 40.9 %all-reduce = (f32[2,128]{1,0:T(2,128)S(1)}, f32[2,128]{1,0:T(2,128)S(1)}) all-reduce(f32[2,128]{1,0:T(2,128)S(1)} %get-tuple-element.279, f32[2,128]{1,0:T(2,128)S(1)} %get-tuple-element.278), channel_id=1, replica_groups=mesh['section'=2,'expert'=16] {'section','expert'}, use_global_device_ids=true, to_apply=%region_13.14 | all-reduce | flops 512 | bytes 4096 | tf_op jit(solution)/shard_map/psum | solution.py:122
  324.3 0.6 constant_dynamic-slice_fusion.2
  324.9 0.6 div.62
  (100 shorter events, 7.7 us)
Async XLA Ops:
  7.2 235.2 %copy-start = (bf16[256,3584]{1,0:T(8,128)(2,1)S(1)}, bf16[256,3584]{1,0:T(8,128)(2,1)}, u32[]{:S(2)}) copy-start(bf16[256,3584]{1,0:T(8,128)(2,1)} %param.20) | copy-start | bytes 5505028
  7.2 190.2 %all-reduce.3.cloned.1.call-start = ((), (), s32[]{:S(2)}) async-start(), calls=%async_computation.2 | async-start | bytes 229376 | tf_op jit(solution)/shard_map/psum | solution.py:17
  7.3 235.1 %copy-start.3 = (f32[3584]{0:T(1024)S(1)}, f32[3584]{0:T(1024)}, u32[]{:S(2)}) copy-start(f32[3584]{0:T(1024)} %param.19) | copy-start | bytes 43012
  12.4 20.6 %all-to-all-start = ((bf16[16,4,3584]{2,1,0:T(4,128)(2,1)}), bf16[16,4,3584]{2,1,0:T(4,128)(2,1)S(1)}, u32[]{:S(2)}, u32[]{:S(2)}) async-start(bf16[16,4,3584]{2,1,0:T(4,128)(2,1)} %bitcast.77), calls=%async_computation | async-start | bytes 917504 | tf_op jit(solution)/shard_map/while/body/eval_jaxpr/all_to_all | solution.py:77
  41.4 17.0 %all-to-all-start.1 = ((bf16[16,4,3584]{2,1,0:T(4,128)(2,1)}), bf16[16,4,3584]{2,1,0:T(4,128)(2,1)S(1)}, u32[]{:S(2)}, u32[]{:S(2)}) async-start(bf16[16,4,3584]{2,1,0:T(4,128)(2,1)} %reshape.219), calls=%async_computation.1 | async-start | bytes 917504 | tf_op jit(solution)/shard_map/while/body/eval_jaxpr/all_to_all | solution.py:49
  59.9 5.2 %collective-permute-start = (bf16[8,3584]{1,0:T(8,128)(2,1)S(1)}, bf16[8,3584]{1,0:T(8,128)(2,1)S(1)}, u32[]{:S(2)}, u32[]{:S(2)}) collective-permute-start(bf16[8,3584]{1,0:T(8,128)(2,1)S(1)} %get-tuple-element.401), channel_id=1, source_target_pairs={{0,16},{1,17},{2,18},{3,19},{4,20},{5,21},{6,22},{7,23},{8,24},{9,... | collective-permute-start | bytes 172040 | tf_op jit(solution)/shard_map/while/body/eval_jaxpr/ppermute | solution.py:12
  70.1 17.0 %all-to-all-start = ((bf16[16,4,3584]{2,1,0:T(4,128)(2,1)}), bf16[16,4,3584]{2,1,0:T(4,128)(2,1)S(1)}, u32[]{:S(2)}, u32[]{:S(2)}) async-start(bf16[16,4,3584]{2,1,0:T(4,128)(2,1)} %bitcast.77), calls=%async_computation | async-start | bytes 917504 | tf_op jit(solution)/shard_map/while/body/eval_jaxpr/all_to_all | solution.py:77
  95.6 17.0 %all-to-all-start.1 = ((bf16[16,4,3584]{2,1,0:T(4,128)(2,1)}), bf16[16,4,3584]{2,1,0:T(4,128)(2,1)S(1)}, u32[]{:S(2)}, u32[]{:S(2)}) async-start(bf16[16,4,3584]{2,1,0:T(4,128)(2,1)} %reshape.219), calls=%async_computation.1 | async-start | bytes 917504 | tf_op jit(solution)/shard_map/while/body/eval_jaxpr/all_to_all | solution.py:49
  114.1 6.1 %collective-permute-start = (bf16[8,3584]{1,0:T(8,128)(2,1)S(1)}, bf16[8,3584]{1,0:T(8,128)(2,1)S(1)}, u32[]{:S(2)}, u32[]{:S(2)}) collective-permute-start(bf16[8,3584]{1,0:T(8,128)(2,1)S(1)} %get-tuple-element.401), channel_id=1, source_target_pairs={{0,16},{1,17},{2,18},{3,19},{4,20},{5,21},{6,22},{7,23},{8,24},{9,... | collective-permute-start | bytes 172040 | tf_op jit(solution)/shard_map/while/body/eval_jaxpr/ppermute | solution.py:12
  125.2 17.0 %all-to-all-start = ((bf16[16,4,3584]{2,1,0:T(4,128)(2,1)}), bf16[16,4,3584]{2,1,0:T(4,128)(2,1)S(1)}, u32[]{:S(2)}, u32[]{:S(2)}) async-start(bf16[16,4,3584]{2,1,0:T(4,128)(2,1)} %bitcast.77), calls=%async_computation | async-start | bytes 917504 | tf_op jit(solution)/shard_map/while/body/eval_jaxpr/all_to_all | solution.py:77
  150.6 17.0 %all-to-all-start.1 = ((bf16[16,4,3584]{2,1,0:T(4,128)(2,1)}), bf16[16,4,3584]{2,1,0:T(4,128)(2,1)S(1)}, u32[]{:S(2)}, u32[]{:S(2)}) async-start(bf16[16,4,3584]{2,1,0:T(4,128)(2,1)} %reshape.219), calls=%async_computation.1 | async-start | bytes 917504 | tf_op jit(solution)/shard_map/while/body/eval_jaxpr/all_to_all | solution.py:49
  169.1 6.1 %collective-permute-start = (bf16[8,3584]{1,0:T(8,128)(2,1)S(1)}, bf16[8,3584]{1,0:T(8,128)(2,1)S(1)}, u32[]{:S(2)}, u32[]{:S(2)}) collective-permute-start(bf16[8,3584]{1,0:T(8,128)(2,1)S(1)} %get-tuple-element.401), channel_id=1, source_target_pairs={{0,16},{1,17},{2,18},{3,19},{4,20},{5,21},{6,22},{7,23},{8,24},{9,... | collective-permute-start | bytes 172040 | tf_op jit(solution)/shard_map/while/body/eval_jaxpr/ppermute | solution.py:12
  175.9 64.5 %all-gather.2.cloned.1.call-start = ((), (), s32[]{:S(2)}) async-start(), calls=%async_computation.3 | async-start | bytes 1949696 | tf_op jit(solution)/shard_map/all_gather | solution.py:110
  197.4 85.6 %copy-start.1 = (s32[2,128]{1,0:T(2,128)S(1)}, s32[2,128]{1,0:T(2,128)}, u32[]{:S(2)}) copy-start(s32[2,128]{1,0:T(2,128)} %param.22) | copy-start | bytes 3076
  197.4 126.7 %copy-start.2 = (s32[2,128]{1,0:T(2,128)S(1)}, s32[2,128]{1,0:T(2,128)}, u32[]{:S(2)}) copy-start(s32[2,128]{1,0:T(2,128)} %param.23) | copy-start | bytes 3076
Sparse Core Ops, SparseCore 0:
  176.0 21.3 all-reduce.2
  199.7 40.6 all-gather.1
where the time goes:
time: 334 us; the launch traced here: 332 us
  waiting for transfers between devices  141 us (42%)
  blocking collectives  79.3 us (24%)
  starting transfers between devices  38.5 us (12%)
  matrix products  28 us (8%)
  other arithmetic  16 us (5%)
  local copies, waits for them, and re-layouts  15.4 us (5%)
  between operations  14.1 us (4%)
    all_gather x1, waiting for transfers between devices, body(): lax.all_gather(shared, 'expert', axis=1, tiled=True)  42.9 us
    psum x1, blocking collectives, body(): lax.psum((local_sum, target_part), ('section', 'expert'))  40.9 us
    all_to_all x3, waiting for transfers between devices, expert_rows(): lax.all_to_all(partial_value.reshape(sources, slot_count, width_in), 'exp...  39.2 us
    pmax x1, blocking collectives, body(): peak = lax.pmax(local_max, ('section', 'expert'))  38.4 us
    all_to_all x3, waiting for transfers between devices, expert_layer(): lax.all_to_all(outgoing, 'expert', split_axis=0, concat_axis=0, tiled=True)  31.6 us
    psum x1, waiting for transfers between devices, broadcast(): return lax.psum(block, axis)  21.4 us
    all_to_all x3, starting transfers between devices, expert_layer(): lax.all_to_all(outgoing, 'expert', split_axis=0, concat_axis=0, tiled=True)  15 us
    dot_general x3, matrix products, expert_rows(): jnp.dot(inner, w_down[0], preferred_element_type=jnp.float32)  13.8 us
  transfers between devices with their start and end apart: 11, of which 11 were waited for; matrix products, arithmetic and copies ran while one was open for 3% of the time, Pallas kernels for 0%

commit v1 on v0

--- a/solution.py
+++ b/solution.py
@@ -4,6 +4,18 @@
 from jax.sharding import PartitionSpec as P
 
 SEQS = 4
+
+
+def gather_by_bits(x, axis, dim):
+    ways, here, lap = (lax.axis_size(axis), lax.axis_index(axis), x.shape[dim])
+    line, have = (x, 1)
+    while have < ways:
+        line = jnp.concatenate(
+            [line, lax.ppermute(line, axis, [(d, (d - have) % ways) for d in range(ways)])],
+            axis=dim,
+        )
+        have = 2 * have
+    return jnp.roll(line, here * lap, axis=dim)
 
 
 def shifted(shard, axis, by):
@@ -107,9 +119,7 @@
     start_record = jnp.zeros((micro_count, tok_count, model_width), jnp.bfloat16)
     arrived, record = lax.fori_loop(0, tick_count, advance, (start_rows, start_record))
     shared = broadcast(record, "section", sections - 1)
-    normed = rms_scale(lax.all_gather(shared, "expert", axis=1, tiled=True), final_gain).astype(
-        jnp.bfloat16
-    )
+    normed = rms_scale(gather_by_bits(shared, "expert", 1), final_gain).astype(jnp.bfloat16)
     logits = jnp.einsum("mrd,vd->mrv", normed, head, preferred_element_type=jnp.float32)
     voc_count = head.shape[0]
     vocab_start = (section_pos * members + member_pos) * voc_count

time: 334 us -> 359 us (1.075)
  waiting for transfers between devices: 141 us -> 158 us
  starting transfers between devices: 38.5 us -> 45.1 us
    ppermute x0 -> x4, waiting for transfers between devices: none -> 60.4 us  [gather_by_bits(): lax.ppermute(line, axis, [(d, (d - have) % ways) for d in range(ways)])]
    all_gather x1 -> x0, waiting for transfers between devices: 42.9 us -> none  [body(): lax.all_gather(shared, 'expert', axis=1, tiled=True)]
    ppermute x0 -> x4, starting transfers between devices: none -> 6.73 us  [gather_by_bits(): lax.ppermute(line, axis, [(d, (d - have) % ways) for d in range(ways)])]
  transfers between devices with their start and end apart: 11 -> 14, of which waited for: 11 -> 14; matrix products, arithmetic and copies ran while one was open for 3% -> 3% of each run, Pallas kernels for 0% -> 0%
where the time goes in v1:
time: 359 us; the launch traced here: 357 us
  waiting for transfers between devices  158 us (44%)
  blocking collectives  78.9 us (22%)
  starting transfers between devices  45.1 us (13%)
  matrix products  26.5 us (7%)
  other arithmetic  17.3 us (5%)
  local copies, waits for them, and re-layouts  16.6 us (5%)
  between operations  14.2 us (4%)
    ppermute x4, waiting for transfers between devices, gather_by_bits(): lax.ppermute(line, axis, [(d, (d - have) % ways) for d in range(ways)])  60.4 us
    psum x1, blocking collectives, body(): lax.psum((local_sum, target_part), ('section', 'expert'))  41.5 us
    all_to_all x3, waiting for transfers between devices, expert_rows(): lax.all_to_all(partial_value.reshape(sources, slot_count, width_in), 'exp...  39.2 us
    pmax x1, blocking collectives, body(): peak = lax.pmax(local_max, ('section', 'expert'))  37.3 us
    all_to_all x3, waiting for transfers between devices, expert_layer(): lax.all_to_all(outgoing, 'expert', split_axis=0, concat_axis=0, tiled=True)  31.6 us
    psum x1, waiting for transfers between devices, broadcast(): return lax.psum(block, axis)  21.5 us
    all_to_all x3, starting transfers between devices, expert_layer(): lax.all_to_all(outgoing, 'expert', split_axis=0, concat_axis=0, tiled=True)  15 us
    dot_general x3, matrix products, expert_rows(): jnp.dot(inner, w_down[0], preferred_element_type=jnp.float32)  13.8 us
  transfers between devices with their start and end apart: 14, of which 14 were waited for; matrix products, arithmetic and copies ran while one was open for 3% of the time, Pallas kernels for 0%

profile of v1, /device:TPU:0, one launch (start us, length us, event | category | flops | bytes accessed | tf_op | source)
XLA Modules:
  0.0 357.1 jit_solution(2149404871257475565)
XLA Ops:
  7.3 168.0 %while.17 = (s32[]{:T(128)}, bf16[8,3584]{1,0:T(8,128)(2,1)S(1)}, bf16[2,8,3584]{2,1,0:T(8,128)(2,1)S(1)}, pred[]{:T(512)}, bf16[2,8,3584]{2,1,0:T(8,128)(2,1)},...) while((s32[]{:T(128)}, bf16[8,3584]{1,0:T(8,128)(2,1)S(1)}, ...), condition=%wide.region_9.10_spmd, body=%wide.region_0.9_spmd.sunk | while | flops 707251328 | bytes 21631636 | solution.py:120
  7.3 0.8 constant_dynamic-slice_fusion.6
  8.7 0.7 multiply_add_fusion.2
  9.5 1.0 fusion.72
  10.5 0.8 reduce.2
  11.5 0.9 broadcast_in_dim.134
  12.4 7.4 %all-to-all-start = ((bf16[16,4,3584]{2,1,0:T(4,128)(2,1)}), bf16[16,4,3584]{2,1,0:T(4,128)(2,1)S(1)}, u32[]{:S(2)}, u32[]{:S(2)}) async-start(bf16[16,4,3584]{2,1,0:T(4,128)(2,1)} %bitcast.77), calls=%async_computation | async-start | bytes 917504 | tf_op jit(solution)/shard_map/while/body/eval_jaxpr/all_to_all | solution.py:89
  20.0 0.7 compare_select_fusion.2
  21.5 0.9 fusion.74
  22.5 10.5 %all-to-all-done = bf16[16,4,3584]{2,1,0:T(4,128)(2,1)S(1)} async-done(((bf16[16,4,3584]{2,1,0:T(4,128)(2,1)}), bf16[16,4,3584]{2,1,0:T(4,128)(2,1)S(1)}, u32[]{:S(2)}, u32[]{:S(2)}) %all-to-all-start) | async-done | bytes 458784 | tf_op jit(solution)/shard_map/while/body/eval_jaxpr/all_to_all | solution.py:89
  33.1 2.8 fusion.73
  35.9 4.6 %convolution_convert_fusion.5 = bf16[64,3584]{1,0:T(8,128)(2,1)S(1)} fusion(bf16[1,512,3584]{2,1,0:T(8,128)(2,1)} %get-tuple-element.450, bf16[64,3584]{1,0:T(8,128)(2,1)S(1)} %reshape.218, bf16[1,3584,512]{2,1,0:T(8,128)(2,1)} %get-tuple-element.449, f32[64,512]{1,0:T(8,128)S(1)} %fusion.73), kind=kOutput, calls=%fused_computation.1.clone.1 | convolution fusion | flops 470188032 | bytes 8388608 | tf_op jit(solution)/shard_map/while/body/eval_jaxpr/dot_general | solution.py:58
  40.5 0.9 reshape.219
  41.4 3.8 %all-to-all-start.1 = ((bf16[16,4,3584]{2,1,0:T(4,128)(2,1)}), bf16[16,4,3584]{2,1,0:T(4,128)(2,1)S(1)}, u32[]{:S(2)}, u32[]{:S(2)}) async-start(bf16[16,4,3584]{2,1,0:T(4,128)(2,1)} %reshape.219), calls=%async_computation.1 | async-start | bytes 917504 | tf_op jit(solution)/shard_map/while/body/eval_jaxpr/all_to_all | solution.py:61
  45.4 13.1 %all-to-all-done.1 = bf16[16,4,3584]{2,1,0:T(4,128)(2,1)S(1)} async-done(((bf16[16,4,3584]{2,1,0:T(4,128)(2,1)}), bf16[16,4,3584]{2,1,0:T(4,128)(2,1)S(1)}, u32[]{:S(2)}, u32[]{:S(2)}) %all-to-all-start.1) | async-done | bytes 458784 | tf_op jit(solution)/shard_map/while/body/eval_jaxpr/all_to_all | solution.py:61
  59.9 3.4 collective-permute-start
  63.4 1.8 collective-permute-done
  66.5 0.7 multiply_add_fusion.2
  67.2 1.0 fusion.72
  68.2 0.8 reduce.2
  69.3 0.9 broadcast_in_dim.134
  70.1 3.8 %all-to-all-start = ((bf16[16,4,3584]{2,1,0:T(4,128)(2,1)}), bf16[16,4,3584]{2,1,0:T(4,128)(2,1)S(1)}, u32[]{:S(2)}, u32[]{:S(2)}) async-start(bf16[16,4,3584]{2,1,0:T(4,128)(2,1)} %bitcast.77), calls=%async_computation | async-start | bytes 917504 | tf_op jit(solution)/shard_map/while/body/eval_jaxpr/all_to_all | solution.py:89
  74.1 0.7 compare_select_fusion.2
  75.0 0.7 fusion.75
  75.7 0.9 fusion.74
  76.6 10.5 %all-to-all-done = bf16[16,4,3584]{2,1,0:T(4,128)(2,1)S(1)} async-done(((bf16[16,4,3584]{2,1,0:T(4,128)(2,1)}), bf16[16,4,3584]{2,1,0:T(4,128)(2,1)S(1)}, u32[]{:S(2)}, u32[]{:S(2)}) %all-to-all-start) | async-done | bytes 458784 | tf_op jit(solution)/shard_map/while/body/eval_jaxpr/all_to_all | solution.py:89
  87.3 2.8 fusion.73
  90.1 4.6 %convolution_convert_fusion.5 = bf16[64,3584]{1,0:T(8,128)(2,1)S(1)} fusion(bf16[1,512,3584]{2,1,0:T(8,128)(2,1)} %get-tuple-element.450, bf16[64,3584]{1,0:T(8,128)(2,1)S(1)} %reshape.218, bf16[1,3584,512]{2,1,0:T(8,128)(2,1)} %get-tuple-element.449, f32[64,512]{1,0:T(8,128)S(1)} %fusion.73), kind=kOutput, calls=%fused_computation.1.clone.1 | convolution fusion | flops 470188032 | bytes 8388608 | tf_op jit(solution)/shard_map/while/body/eval_jaxpr/dot_general | solution.py:58
  94.7 0.9 reshape.219
  95.6 3.8 %all-to-all-start.1 = ((bf16[16,4,3584]{2,1,0:T(4,128)(2,1)}), bf16[16,4,3584]{2,1,0:T(4,128)(2,1)S(1)}, u32[]{:S(2)}, u32[]{:S(2)}) async-start(bf16[16,4,3584]{2,1,0:T(4,128)(2,1)} %reshape.219), calls=%async_computation.1 | async-start | bytes 917504 | tf_op jit(solution)/shard_map/while/body/eval_jaxpr/all_to_all | solution.py:61
  99.5 13.1 %all-to-all-done.1 = bf16[16,4,3584]{2,1,0:T(4,128)(2,1)S(1)} async-done(((bf16[16,4,3584]{2,1,0:T(4,128)(2,1)}), bf16[16,4,3584]{2,1,0:T(4,128)(2,1)S(1)}, u32[]{:S(2)}, u32[]{:S(2)}) %all-to-all-start.1) | async-done | bytes 458784 | tf_op jit(solution)/shard_map/while/body/eval_jaxpr/all_to_all | solution.py:61
  114.1 4.3 %collective-permute-start = (bf16[8,3584]{1,0:T(8,128)(2,1)S(1)}, bf16[8,3584]{1,0:T(8,128)(2,1)S(1)}, u32[]{:S(2)}, u32[]{:S(2)}) collective-permute-start(bf16[8,3584]{1,0:T(8,128)(2,1)S(1)} %get-tuple-element.401), channel_id=1, source_target_pairs={{0,16},{1,17},{2,18},{3,19},{4,20},{5,21},{6,22},{7,23},{8,24},{9,... | collective-permute-start | bytes 172040 | tf_op jit(solution)/shard_map/while/body/eval_jaxpr/ppermute | solution.py:24
  118.4 1.8 collective-permute-done
  121.5 0.7 multiply_add_fusion.2
  122.3 1.0 fusion.72
  123.3 0.8 reduce.2
  124.3 0.9 broadcast_in_dim.134
  125.2 3.8 %all-to-all-start = ((bf16[16,4,3584]{2,1,0:T(4,128)(2,1)}), bf16[16,4,3584]{2,1,0:T(4,128)(2,1)S(1)}, u32[]{:S(2)}, u32[]{:S(2)}) async-start(bf16[16,4,3584]{2,1,0:T(4,128)(2,1)} %bitcast.77), calls=%async_computation | async-start | bytes 917504 | tf_op jit(solution)/shard_map/while/body/eval_jaxpr/all_to_all | solution.py:89
  129.2 0.7 compare_select_fusion.2
  130.7 0.9 fusion.74
  131.7 10.5 %all-to-all-done = bf16[16,4,3584]{2,1,0:T(4,128)(2,1)S(1)} async-done(((bf16[16,4,3584]{2,1,0:T(4,128)(2,1)}), bf16[16,4,3584]{2,1,0:T(4,128)(2,1)S(1)}, u32[]{:S(2)}, u32[]{:S(2)}) %all-to-all-start) | async-done | bytes 458784 | tf_op jit(solution)/shard_map/while/body/eval_jaxpr/all_to_all | solution.py:89
  142.3 2.8 fusion.73
  145.1 4.6 %convolution_convert_fusion.5 = bf16[64,3584]{1,0:T(8,128)(2,1)S(1)} fusion(bf16[1,512,3584]{2,1,0:T(8,128)(2,1)} %get-tuple-element.450, bf16[64,3584]{1,0:T(8,128)(2,1)S(1)} %reshape.218, bf16[1,3584,512]{2,1,0:T(8,128)(2,1)} %get-tuple-element.449, f32[64,512]{1,0:T(8,128)S(1)} %fusion.73), kind=kOutput, calls=%fused_computation.1.clone.1 | convolution fusion | flops 470188032 | bytes 8388608 | tf_op jit(solution)/shard_map/while/body/eval_jaxpr/dot_general | solution.py:58
  149.7 0.9 reshape.219
  150.6 3.8 %all-to-all-start.1 = ((bf16[16,4,3584]{2,1,0:T(4,128)(2,1)}), bf16[16,4,3584]{2,1,0:T(4,128)(2,1)S(1)}, u32[]{:S(2)}, u32[]{:S(2)}) async-start(bf16[16,4,3584]{2,1,0:T(4,128)(2,1)} %reshape.219), calls=%async_computation.1 | async-start | bytes 917504 | tf_op jit(solution)/shard_map/while/body/eval_jaxpr/all_to_all | solution.py:61
  154.6 13.1 %all-to-all-done.1 = bf16[16,4,3584]{2,1,0:T(4,128)(2,1)S(1)} async-done(((bf16[16,4,3584]{2,1,0:T(4,128)(2,1)}), bf16[16,4,3584]{2,1,0:T(4,128)(2,1)S(1)}, u32[]{:S(2)}, u32[]{:S(2)}) %all-to-all-start.1) | async-done | bytes 458784 | tf_op jit(solution)/shard_map/while/body/eval_jaxpr/all_to_all | solution.py:61
  169.1 4.3 %collective-permute-start = (bf16[8,3584]{1,0:T(8,128)(2,1)S(1)}, bf16[8,3584]{1,0:T(8,128)(2,1)S(1)}, u32[]{:S(2)}, u32[]{:S(2)}) collective-permute-start(bf16[8,3584]{1,0:T(8,128)(2,1)S(1)} %get-tuple-element.401), channel_id=1, source_target_pairs={{0,16},{1,17},{2,18},{3,19},{4,20},{5,21},{6,22},{7,23},{8,24},{9,... | collective-permute-start | bytes 172040 | tf_op jit(solution)/shard_map/while/body/eval_jaxpr/ppermute | solution.py:24
  173.4 1.8 collective-permute-done
  175.9 21.5 %all-reduce.3.cloned.1.call-done = bf16[2,8,3584]{2,1,0:T(8,128)(2,1)} async-done(((bf16[2,8,3584]{2,1,0:T(8,128)(2,1)}), bf16[2,8,3584]{2,1,0:T(8,128)(2,1)}) %all-reduce.3.cloned.1.call-update) | async-done | bytes 114704 | tf_op jit(solution)/shard_map/psum | solution.py:29
  197.4 3.2 collective-permute-start.1
  200.6 2.7 collective-permute-done.1
  203.3 0.9 pad_maximum_fusion.2
  204.2 1.2 collective-permute-start.2
  205.4 4.9 %collective-permute-done.2 = bf16[2,16,3584]{2,1,0:T(8,128)(2,1)S(1)} collective-permute-done((bf16[2,16,3584]{2,1,0:T(8,128)(2,1)S(1)}, bf16[2,16,3584]{2,1,0:T(8,128)(2,1)S(1)}, u32[]{:S(2)}, u32[]{:S(2)}) %collective-permute-start.2) | collective-permute-done | bytes 229408 | tf_op jit(solution)/shard_map/ppermute | solution.py:14
  210.3 0.9 pad_maximum_fusion.1
  211.2 0.9 collective-permute-start.3
  212.1 0.9 constant_dynamic-update-slice_fusion.9
  213.0 11.1 %collective-permute-done.3 = bf16[2,32,3584]{2,1,0:T(8,128)(2,1)S(1)} collective-permute-done((bf16[2,32,3584]{2,1,0:T(8,128)(2,1)S(1)}, bf16[2,32,3584]{2,1,0:T(8,128)(2,1)S(1)}, u32[]{:S(2)}, u32[]{:S(2)}) %collective-permute-start.3) | collective-permute-done | bytes 458784 | tf_op jit(solution)/shard_map/ppermute | solution.py:14
  224.2 1.0 pad_maximum_fusion
  225.1 1.5 collective-permute-start.4
  226.7 41.6 %collective-permute-done.4 = bf16[2,64,3584]{2,1,0:T(8,128)(2,1)S(1)} collective-permute-done((bf16[2,64,3584]{2,1,0:T(8,128)(2,1)S(1)}, bf16[2,64,3584]{2,1,0:T(8,128)(2,1)S(1)}, u32[]{:S(2)}, u32[]{:S(2)}) %collective-permute-start.4) | collective-permute-done | bytes 917536 | tf_op jit(solution)/shard_map/ppermute | solution.py:14
  269.1 0.8 fusion.41
  269.9 37.3 %pmax.7 = f32[2,128]{1,0:T(2,128)S(1)} all-reduce(f32[2,128]{1,0:T(2,128)S(1)} %get-tuple-element.314), channel_id=1, replica_groups=mesh['section'=2,'expert'=16] {'section','expert'}, use_global_device_ids=true, to_apply=%region_15.16 | all-reduce | flops 256 | bytes 2048 | tf_op jit(solution)/shard_map/pmax | solution.py:130
  307.4 41.5 %all-reduce = (f32[2,128]{1,0:T(2,128)S(1)}, f32[2,128]{1,0:T(2,128)S(1)}) all-reduce(f32[2,128]{1,0:T(2,128)S(1)} %get-tuple-element.279, f32[2,128]{1,0:T(2,128)S(1)} %get-tuple-element.278), channel_id=1, replica_groups=mesh['section'=2,'expert'=16] {'section','expert'}, use_global_device_ids=true, to_apply=%region_13.14 | all-reduce | flops 512 | bytes 4096 | tf_op jit(solution)/shard_map/psum | solution.py:132
  (120 shorter events, 14.8 us)
Async XLA Ops:
  7.2 261.9 %copy-start = (bf16[256,3584]{1,0:T(8,128)(2,1)S(1)}, bf16[256,3584]{1,0:T(8,128)(2,1)}, u32[]{:S(2)}) copy-start(bf16[256,3584]{1,0:T(8,128)(2,1)} %param.20) | copy-start | bytes 5505028
  7.2 190.2 %all-reduce.3.cloned.1.call-start = ((), (), s32[]{:S(2)}) async-start(), calls=%async_computation.2 | async-start | bytes 229376 | tf_op jit(solution)/shard_map/psum | solution.py:29
  12.4 20.6 %all-to-all-start = ((bf16[16,4,3584]{2,1,0:T(4,128)(2,1)}), bf16[16,4,3584]{2,1,0:T(4,128)(2,1)S(1)}, u32[]{:S(2)}, u32[]{:S(2)}) async-start(bf16[16,4,3584]{2,1,0:T(4,128)(2,1)} %bitcast.77), calls=%async_computation | async-start | bytes 917504 | tf_op jit(solution)/shard_map/while/body/eval_jaxpr/all_to_all | solution.py:89
  41.4 17.0 %all-to-all-start.1 = ((bf16[16,4,3584]{2,1,0:T(4,128)(2,1)}), bf16[16,4,3584]{2,1,0:T(4,128)(2,1)S(1)}, u32[]{:S(2)}, u32[]{:S(2)}) async-start(bf16[16,4,3584]{2,1,0:T(4,128)(2,1)} %reshape.219), calls=%async_computation.1 | async-start | bytes 917504 | tf_op jit(solution)/shard_map/while/body/eval_jaxpr/all_to_all | solution.py:61
  59.9 5.2 %collective-permute-start = (bf16[8,3584]{1,0:T(8,128)(2,1)S(1)}, bf16[8,3584]{1,0:T(8,128)(2,1)S(1)}, u32[]{:S(2)}, u32[]{:S(2)}) collective-permute-start(bf16[8,3584]{1,0:T(8,128)(2,1)S(1)} %get-tuple-element.401), channel_id=1, source_target_pairs={{0,16},{1,17},{2,18},{3,19},{4,20},{5,21},{6,22},{7,23},{8,24},{9,... | collective-permute-start | bytes 172040 | tf_op jit(solution)/shard_map/while/body/eval_jaxpr/ppermute | solution.py:24
  70.1 17.0 %all-to-all-start = ((bf16[16,4,3584]{2,1,0:T(4,128)(2,1)}), bf16[16,4,3584]{2,1,0:T(4,128)(2,1)S(1)}, u32[]{:S(2)}, u32[]{:S(2)}) async-start(bf16[16,4,3584]{2,1,0:T(4,128)(2,1)} %bitcast.77), calls=%async_computation | async-start | bytes 917504 | tf_op jit(solution)/shard_map/while/body/eval_jaxpr/all_to_all | solution.py:89
  95.6 17.0 %all-to-all-start.1 = ((bf16[16,4,3584]{2,1,0:T(4,128)(2,1)}), bf16[16,4,3584]{2,1,0:T(4,128)(2,1)S(1)}, u32[]{:S(2)}, u32[]{:S(2)}) async-start(bf16[16,4,3584]{2,1,0:T(4,128)(2,1)} %reshape.219), calls=%async_computation.1 | async-start | bytes 917504 | tf_op jit(solution)/shard_map/while/body/eval_jaxpr/all_to_all | solution.py:61
  114.1 6.1 %collective-permute-start = (bf16[8,3584]{1,0:T(8,128)(2,1)S(1)}, bf16[8,3584]{1,0:T(8,128)(2,1)S(1)}, u32[]{:S(2)}, u32[]{:S(2)}) collective-permute-start(bf16[8,3584]{1,0:T(8,128)(2,1)S(1)} %get-tuple-element.401), channel_id=1, source_target_pairs={{0,16},{1,17},{2,18},{3,19},{4,20},{5,21},{6,22},{7,23},{8,24},{9,... | collective-permute-start | bytes 172040 | tf_op jit(solution)/shard_map/while/body/eval_jaxpr/ppermute | solution.py:24
  125.2 17.0 %all-to-all-start = ((bf16[16,4,3584]{2,1,0:T(4,128)(2,1)}), bf16[16,4,3584]{2,1,0:T(4,128)(2,1)S(1)}, u32[]{:S(2)}, u32[]{:S(2)}) async-start(bf16[16,4,3584]{2,1,0:T(4,128)(2,1)} %bitcast.77), calls=%async_computation | async-start | bytes 917504 | tf_op jit(solution)/shard_map/while/body/eval_jaxpr/all_to_all | solution.py:89
  150.6 17.0 %all-to-all-start.1 = ((bf16[16,4,3584]{2,1,0:T(4,128)(2,1)}), bf16[16,4,3584]{2,1,0:T(4,128)(2,1)S(1)}, u32[]{:S(2)}, u32[]{:S(2)}) async-start(bf16[16,4,3584]{2,1,0:T(4,128)(2,1)} %reshape.219), calls=%async_computation.1 | async-start | bytes 917504 | tf_op jit(solution)/shard_map/while/body/eval_jaxpr/all_to_all | solution.py:61
  169.1 6.1 %collective-permute-start = (bf16[8,3584]{1,0:T(8,128)(2,1)S(1)}, bf16[8,3584]{1,0:T(8,128)(2,1)S(1)}, u32[]{:S(2)}, u32[]{:S(2)}) collective-permute-start(bf16[8,3584]{1,0:T(8,128)(2,1)S(1)} %get-tuple-element.401), channel_id=1, source_target_pairs={{0,16},{1,17},{2,18},{3,19},{4,20},{5,21},{6,22},{7,23},{8,24},{9,... | collective-permute-start | bytes 172040 | tf_op jit(solution)/shard_map/while/body/eval_jaxpr/ppermute | solution.py:24
  197.4 71.0 %copy-start.1 = (bf16[2,8,3584]{2,1,0:T(8,128)(2,1)S(1)}, bf16[2,8,3584]{2,1,0:T(8,128)(2,1)}, u32[]{:S(2)}) copy-start(bf16[2,8,3584]{2,1,0:T(8,128)(2,1)} %all-reduce.3.cloned.1.call-done) | copy-start | bytes 344068
  197.4 5.9 %collective-permute-start.1 = (bf16[2,8,3584]{2,1,0:T(8,128)(2,1)}, bf16[2,8,3584]{2,1,0:T(8,128)(2,1)S(1)}, u32[]{:S(2)}, u32[]{:S(2)}) collective-permute-start(bf16[2,8,3584]{2,1,0:T(8,128)(2,1)} %all-reduce.3.cloned.1.call-done), channel_id=1, source_target_pairs={{0,15},{1,0},{2,1},{3,2},{4,3},{5,4},{6,5},{7,6},{8,7},{9,8},{10,9... | collective-permute-start | bytes 344072 | tf_op jit(solution)/shard_map/ppermute | solution.py:14
  204.2 6.1 %collective-permute-start.2 = (bf16[2,16,3584]{2,1,0:T(8,128)(2,1)S(1)}, bf16[2,16,3584]{2,1,0:T(8,128)(2,1)S(1)}, u32[]{:S(2)}, u32[]{:S(2)}) collective-permute-start(bf16[2,16,3584]{2,1,0:T(8,128)(2,1)S(1)} %pad_maximum_fusion.2), channel_id=1, source_target_pairs={{0,14},{1,15},{2,0},{3,1},{4,2},{5,3},{6,4},{7,5},{8,6},{9,7},{10,... | collective-permute-start | bytes 688136 | tf_op jit(solution)/shard_map/ppermute | solution.py:14
  211.2 12.9 %collective-permute-start.3 = (bf16[2,32,3584]{2,1,0:T(8,128)(2,1)S(1)}, bf16[2,32,3584]{2,1,0:T(8,128)(2,1)S(1)}, u32[]{:S(2)}, u32[]{:S(2)}) collective-permute-start(bf16[2,32,3584]{2,1,0:T(8,128)(2,1)S(1)} %pad_maximum_fusion.1), channel_id=1, source_target_pairs={{0,12},{1,13},{2,14},{3,15},{4,0},{5,1},{6,2},{7,3},{8,4},{9,5},{1... | collective-permute-start | bytes 1376264 | tf_op jit(solution)/shard_map/ppermute | solution.py:14
  225.1 43.2 %collective-permute-start.4 = (bf16[2,64,3584]{2,1,0:T(8,128)(2,1)S(1)}, bf16[2,64,3584]{2,1,0:T(8,128)(2,1)S(1)}, u32[]{:S(2)}, u32[]{:S(2)}) collective-permute-start(bf16[2,64,3584]{2,1,0:T(8,128)(2,1)S(1)} %pad_maximum_fusion), channel_id=1, source_target_pairs={{0,8},{1,9},{2,10},{3,11},{4,12},{5,13},{6,14},{7,15},{8,0},{9,1},... | collective-permute-start | bytes 2752520 | tf_op jit(solution)/shard_map/ppermute | solution.py:14
  226.7 42.4 %copy-start.4 = (f32[3584]{0:T(1024)S(1)}, f32[3584]{0:T(1024)}, u32[]{:S(2)}) copy-start(f32[3584]{0:T(1024)} %param.19) | copy-start | bytes 43012
  268.6 38.6 %copy-start.2 = (s32[2,128]{1,0:T(2,128)S(1)}, s32[2,128]{1,0:T(2,128)}, u32[]{:S(2)}) copy-start(s32[2,128]{1,0:T(2,128)} %param.22) | copy-start | bytes 3076
  268.6 80.4 %copy-start.3 = (s32[2,128]{1,0:T(2,128)S(1)}, s32[2,128]{1,0:T(2,128)}, u32[]{:S(2)}) copy-start(s32[2,128]{1,0:T(2,128)} %param.23) | copy-start | bytes 3076
Sparse Core Ops, SparseCore 0:
  176.0 21.3 all-reduce.2
